TPU v7x, 32 devices: a whole 2x2x4 slice. The times are simulated.
32 devices in a mesh: rep: 4 (over y, x), shard: 8 (over z, core).
Axes of the slice: x: 2, y: 2, z: 4, core: 2. Of those that a mesh axis runs over, the one named last changes fastest.
Arguments:
- hot_ids: int32 [65536], P(('rep', 'shard')), may hold values from 0 to 8191
- hot_grads: bfloat16 [65536, 128], P(('rep', 'shard')), may hold values from -6 to 6
- hot_rows: float32 [8192, 128], replicated, may hold values from -6 to 6
- hot_accum: float32 [8192], replicated, may hold values from 0.5 to 4
- cold_counts: int32 [32, 32], P(('rep', 'shard')), may hold values from 1 to 16, as said below
- cold_slots: int32 [32, 32, 16], P(('rep', 'shard')), may hold values from 0 to 8191
- cold_grads: bfloat16 [32, 32, 16, 128], P(('rep', 'shard')), may hold values from -6 to 6
- cold_rows: float32 [262144, 128], P(('rep', 'shard')), may hold values from -6 to 6
- cold_accum: float32 [262144], P(('rep', 'shard')), may hold values from 0.5 to 4
Outputs:
- new_hot_rows: float32 [8192, 128], replicated
- new_hot_accum: float32 [8192], replicated
- new_cold_rows: float32 [262144, 128], P(('rep', 'shard'))
- new_cold_accum: float32 [262144], P(('rep', 'shard'))
Inputs may be any that keep to these rules, and one draw needn't show every extreme that they name: `cold_counts`: every entry is at least 1 and at most 16; in every draw some owner receives 16 live slots from every sender.
All inputs are finite; a program needn't handle non-finite values.
Results may differ from a plain program's by a relative error of at most 0.0003.
Values may be sent and summed in bfloat16 or wider, within the bound.
A program may use at most 128 MiB of HBM per device.

v0:
```python
import jax
import jax.numpy as jnp
from jax import lax
from jax.sharding import PartitionSpec as P

learn_rate = 0.5


def adagrad(table_rows, accum_rows, gradient):
    accum_new = accum_rows + jnp.mean(gradient * gradient, axis=1)
    return (table_rows - learn_rate * gradient / jnp.sqrt(accum_new)[:, None], accum_new)


def local(
    hot_ids,
    hot_grads,
    hot_rows,
    hot_accum,
    cold_counts,
    cold_slots,
    cold_grads,
    cold_rows,
    cold_accum,
):
    hot_count = hot_rows.shape[0]
    dense = jax.ops.segment_sum(hot_grads.astype(jnp.float32), hot_ids, num_segments=hot_count)
    share = hot_count // lax.axis_size("shard")
    part_sum = lax.psum_scatter(dense, "shard", scatter_dimension=0, tiled=True)
    part_sum = lax.psum(part_sum, "rep")
    start = lax.axis_index("shard") * share
    rows_share = lax.dynamic_slice_in_dim(hot_rows, start, share, 0)
    accum_share = lax.dynamic_slice_in_dim(hot_accum, start, share, 0)
    rows_new, accum_new = adagrad(rows_share, accum_share, part_sum)
    new_hot_rows, new_hot_accum = (
        lax.all_gather(rows_new, "shard", axis=0, tiled=True),
        lax.all_gather(accum_new, "shard", axis=0, tiled=True),
    )
    received, slots_in, counts_in = (
        lax.all_to_all(cold_grads, ("rep", "shard"), split_axis=1, concat_axis=0, tiled=True),
        lax.all_to_all(cold_slots, ("rep", "shard"), split_axis=1, concat_axis=0, tiled=True),
        lax.all_to_all(cold_counts, ("rep", "shard"), split_axis=1, concat_axis=0, tiled=True),
    )
    width = received.shape[-1]
    capacity = received.shape[2]
    slot_index = lax.broadcasted_iota(jnp.int32, (1, 1, capacity), 2)
    live_mask = slot_index < counts_in[:, :, None]
    masked_terms = jnp.where(live_mask[..., None], received.astype(jnp.float32), 0.0)
    local_rows = cold_rows.shape[0]
    cold_sum = jax.ops.segment_sum(
        masked_terms.reshape(-1, width), slots_in.reshape(-1), num_segments=local_rows
    )
    new_cold_rows, new_cold_accum = adagrad(cold_rows, cold_accum, cold_sum)
    return (new_hot_rows, new_hot_accum, new_cold_rows, new_cold_accum)


def solution(mesh):
    placed = (
        P(("rep", "shard")),
        P(("rep", "shard"), None),
        P(),
        P(),
        P(("rep", "shard"), None),
        P(("rep", "shard"), None, None),
        P(("rep", "shard"), None, None, None),
        P(("rep", "shard"), None),
        P(("rep", "shard")),
    )
    return jax.shard_map(
        local,
        mesh=mesh,
        in_specs=placed,
        out_specs=(P(), P(), P(("rep", "shard"), None), P(("rep", "shard"))),
        check_vma=False,
    )
```

profile of v0, /device:TPU:0, one launch (start us, length us, event | category | flops | bytes accessed | tf_op | source)
XLA Modules:
  0.0 199.6 jit_solution(5830766798041887270)
XLA Ops:
  7.2 0.0 reduce-scatter.2.cloned.1.call-start
  7.2 14.1 %scatter_custom_fusion = f32[8192,128]{1,0:T(8,128)} fusion(s32[2048]{0:T(1024)} %param.9, f32[]{:T(128)} %constant.3.clone.1, bf16[2048,128]{1,0:T(8,128)(2,1)} %param.10), kind=kCustom, calls=%fused_computation.6 | custom fusion | flops 524288 | bytes 4719104 | tf_op jit(solution)/shard_map/scatter-add | solution.py:26
  21.3 0.0 reduce-scatter.2.cloned.1.call-update
  21.3 0.0 all-reduce.2.cloned.1.call-start
  21.4 52.8 %reduce-scatter.2.cloned.1.call-done = f32[1024,128]{1,0:T(8,128)} async-done(((f32[8192,128]{1,0:T(8,128)}), f32[1024,128]{1,0:T(8,128)}) %reduce-scatter.2.cloned.1.call-update) | async-done | bytes 524304 | tf_op jit(solution)/shard_map/reduce_scatter | solution.py:28
  74.1 0.0 all-reduce.2.cloned.1.call-update
  74.2 0.0 all-gather.2.cloned.1.call-start
  74.2 46.8 %all-reduce.2.cloned.1.call-done = f32[1024,128]{1,0:T(8,128)} async-done(((f32[1024,128]{1,0:T(8,128)}), f32[1024,128]{1,0:T(8,128)}) %all-reduce.2.cloned.1.call-update) | async-done | bytes 524304 | tf_op jit(solution)/shard_map/psum | solution.py:29
  121.0 1.2 multiply_reduce_fusion.1
  122.2 0.7 fusion.8
  122.9 2.2 %divide_subtract_fusion.1 = f32[1024,128]{1,0:T(8,128)} fusion(f32[1024,128]{1,0:T(8,128)} %all-reduce.2.cloned.1.call-done, f32[8192,128]{1,0:T(8,128)} %param.11, s32[]{:T(128)S(6)} %select_n.11, f32[1024]{0:T(1024)S(1)} %get-tuple-element.6), kind=kLoop, calls=%fused_computation.9 | loop fusion | flops 393216 | bytes 1576964 | tf_op jit(solution)/shard_map/sub | solution.py:11
  125.1 0.0 all-gather.2.cloned.1.call-update
  125.2 0.7 copy.18
  125.9 4.6 %all-to-all-start.1 = ((s32[1,32,1]{2,0,1:T(1,128)}), s32[1,32,1]{2,0,1:T(1,128)S(1)}, u32[]{:S(2)}, u32[]{:S(2)}) async-start(s32[1,32,1]{2,0,1:T(1,128)} %copy.18), calls=%async_computation.2 | async-start | bytes 32768 | tf_op jit(solution)/shard_map/all_to_all | solution.py:41
  130.5 0.1 copy.17
  130.6 7.0 %all-to-all-done.1 = s32[1,32,1]{2,0,1:T(1,128)S(1)} async-done(((s32[1,32,1]{2,0,1:T(1,128)}), s32[1,32,1]{2,0,1:T(1,128)S(1)}, u32[]{:S(2)}, u32[]{:S(2)}) %all-to-all-start.1) | async-done | bytes 160 | tf_op jit(solution)/shard_map/all_to_all | solution.py:41
  137.6 9.1 %all_to_all.31 = s32[1,32,16]{2,0,1:T(1,128)S(1)} all-to-all(s32[1,32,16]{2,0,1:T(1,128)S(1)} %copy.17), channel_id=1, replica_groups=mesh['rep'=4,'shard'=8] {'rep','shard'}, dimensions={1} | all-to-all | bytes 4096 | tf_op jit(solution)/shard_map/all_to_all | solution.py:40
  146.7 2.6 %all-to-all-start.2 = ((bf16[1,32,16,128]{3,2,0,1:T(8,128)(2,1)}), bf16[1,32,16,128]{3,2,0,1:T(8,128)(2,1)S(1)}, u32[]{:S(2)}, u32[]{:S(2)}) async-start(bf16[1,32,16,128]{3,2,0,1:T(8,128)(2,1)} %bitcast.1), calls=%async_computation.3 | async-start | bytes 262144 | tf_op jit(solution)/shard_map/all_to_all | solution.py:39
  149.3 0.7 reduce.1
  150.0 0.1 iota_compare_fusion
  150.0 0.1 lt.33
  150.1 0.5 broadcast.40
  150.6 0.7 reduce.4
  151.3 0.1 reshape.77
  151.4 9.5 %all-to-all-done.2 = bf16[1,32,16,128]{3,2,0,1:T(8,128)(2,1)S(1)} async-done(((bf16[1,32,16,128]{3,2,0,1:T(8,128)(2,1)}), bf16[1,32,16,128]{3,2,0,1:T(8,128)(2,1)S(1)}, u32[]{:S(2)}, u32[]{:S(2)}) %all-to-all-start.2) | async-done | bytes 131104 | tf_op jit(solution)/shard_map/all_to_all | solution.py:39
  160.9 4.6 %scatter_custom_fusion.1 = f32[8192,128]{1,0:T(8,128)} fusion(s32[512]{0:T(512)S(1)} %reshape.77, f32[]{:T(128)} %constant.3.clone.1, bf16[512,128]{1,0:T(8,128)(2,1)S(1)} %bitcast.7, pred[512]{0:T(512)(128)(4,1)S(1)} %lt.33), kind=kCustom, calls=%fused_computation.4 | custom fusion | flops 196608 | bytes 4326912 | tf_op jit(solution)/shard_map/scatter-add | solution.py:49
  165.5 3.5 %multiply_reduce_fusion = f32[8192]{0:T(1024)S(1)} fusion(f32[8192,128]{1,0:T(8,128)} %scatter_custom_fusion.1), kind=kLoop, calls=%fused_computation.3 | loop fusion | flops 2088960 | bytes 4227072 | tf_op jit(solution)/shard_map/reduce_sum | solution.py:10
  169.1 0.6 fusion.7
  169.7 4.2 %divide_subtract_fusion = f32[8192,128]{1,0:T(8,128)} fusion(f32[8192,128]{1,0:T(8,128)} %param.16, f32[8192,128]{1,0:T(8,128)S(1)} %copy-done, f32[8192]{0:T(1024)S(1)} %get-tuple-element.4), kind=kLoop, calls=%fused_computation.2 | loop fusion | flops 3145728 | bytes 12615680 | tf_op jit(solution)/shard_map/sub | solution.py:11
  173.9 14.1 %all_gather.7 = f32[8192]{0:T(1024)S(1)} all-gather(f32[1024]{0:T(1024)S(1)} %get-tuple-element.7), channel_id=1, replica_groups=mesh['rep'=4,'shard'=8] {'shard'}, dimensions={0}, use_global_device_ids=true | all-gather | bytes 36864 | tf_op jit(solution)/shard_map/all_gather | solution.py:36
  188.0 4.5 %copy.23 = f32[8192,128]{1,0:T(8,128)} copy(f32[8192,128]{1,0:T(8,128)} %all-gather.2.cloned.1.call-done) | data formatting | bytes 8388608
  192.4 0.6 copy.24
  (9 shorter events, 0.0 us)
Async XLA Ops:
  7.2 67.0 %reduce-scatter.2.cloned.1.call-start = ((), (), s32[]{:S(2)}) async-start(), calls=%async_computation.4 | async-start | bytes 4718592 | tf_op jit(solution)/shard_map/reduce_scatter | solution.py:28
  21.3 103.9 %copy-start.3 = (s32[1,32]{1,0:T(1,128)S(1)}, s32[1,32]{1,0:T(1,128)}, u32[]{:S(2)}) copy-start(s32[1,32]{1,0:T(1,128)} %param.13) | copy-start | bytes 388
  21.3 109.2 %copy-start.2 = (s32[1,32,16]{1,2,0:T(8,128)S(1)}, s32[1,32,16]{1,2,0:T(8,128)}, u32[]{:S(2)}) copy-start(s32[1,32,16]{1,2,0:T(8,128)} %param.14) | copy-start | bytes 6148
  21.3 99.7 %all-reduce.2.cloned.1.call-start = ((), (), s32[]{:S(2)}) async-start(), calls=%async_computation.5 | async-start | bytes 1048576 | tf_op jit(solution)/shard_map/psum | solution.py:29
  74.2 113.8 %all-gather.2.cloned.1.call-start = ((), (), s32[]{:S(2)}) async-start(), calls=%async_computation.6 | async-start | bytes 4718592 | tf_op jit(solution)/shard_map/all_gather | solution.py:35
  125.9 11.7 %all-to-all-start.1 = ((s32[1,32,1]{2,0,1:T(1,128)}), s32[1,32,1]{2,0,1:T(1,128)S(1)}, u32[]{:S(2)}, u32[]{:S(2)}) async-start(s32[1,32,1]{2,0,1:T(1,128)} %copy.18), calls=%async_computation.2 | async-start | bytes 32768 | tf_op jit(solution)/shard_map/all_to_all | solution.py:41
  146.7 14.2 %all-to-all-start.2 = ((bf16[1,32,16,128]{3,2,0,1:T(8,128)(2,1)}), bf16[1,32,16,128]{3,2,0,1:T(8,128)(2,1)S(1)}, u32[]{:S(2)}, u32[]{:S(2)}) async-start(bf16[1,32,16,128]{3,2,0,1:T(8,128)(2,1)} %bitcast.1), calls=%async_computation.3 | async-start | bytes 262144 | tf_op jit(solution)/shard_map/all_to_all | solution.py:39
  160.9 8.1 %copy-start.1 = (f32[8192]{0:T(1024)S(1)}, f32[8192]{0:T(1024)}, u32[]{:S(2)}) copy-start(f32[8192]{0:T(1024)} %param.17) | copy-start | bytes 98308
  165.5 4.1 %copy-start = (f32[8192,128]{1,0:T(8,128)S(1)}, f32[8192,128]{1,0:T(8,128)}, u32[]{:S(2)}) copy-start(f32[8192,128]{1,0:T(8,128)} %scatter_custom_fusion.1) | copy-start | bytes 12582916
Sparse Core Ops, SparseCore 0:
  21.4 52.6 reduce-scatter.1
  77.1 43.8 all-reduce.1
  125.3 50.0 all-gather.1
where the time goes:
time: 200 us
  waiting for transfers between devices  116 us (58%)
  other arithmetic  32.6 us (16%)
  blocking collectives  23.2 us (12%)
  between operations  13.8 us (7%)
  starting transfers between devices  7.29 us (4%)
  local copies, waits for them, and re-layouts  6.56 us (3%)
    reduce_scatter x1, waiting for transfers between devices, local(): part_sum = lax.psum_scatter(dense, 'shard', scatter_dimension=0, tiled=True)  52.8 us
    psum x1, waiting for transfers between devices, local(): part_sum = lax.psum(part_sum, 'rep')  46.8 us
    scatter-add x1, other arithmetic, local(): jax.ops.segment_sum(hot_grads.astype(jnp.float32), hot_ids, num_segments=...  14.1 us
    all_gather x1, blocking collectives, local(): lax.all_gather(accum_new, 'shard', axis=0, tiled=True)  14.1 us
    all_to_all x1, waiting for transfers between devices, local(): lax.all_to_all(cold_grads, ('rep', 'shard'), split_axis=1, concat_axis=0,...  9.51 us
    all_to_all x1, blocking collectives, local(): lax.all_to_all(cold_slots, ('rep', 'shard'), split_axis=1, concat_axis=0,...  9.13 us
    all_to_all x1, waiting for transfers between devices, local(): lax.all_to_all(cold_counts, ('rep', 'shard'), split_axis=1, concat_axis=0...  7.01 us
    sub x2, other arithmetic, adagrad(): table_rows - learn_rate * gradient / jnp.sqrt(accum_new)[:, None]  6.43 us
  transfers between devices with their start and end apart: 5, of which 4 were waited for; matrix products, arithmetic and copies ran while one was open for 8% of the time, Pallas kernels for 0%

commit v1 on v0

--- a/solution.py
+++ b/solution.py
@@ -1,9 +1,24 @@
+import functools
 import jax
 import jax.numpy as jnp
 from jax import lax
 from jax.sharding import PartitionSpec as P
 
 learn_rate = 0.5
+
+
+def build_stocks_over_axis(vec, across):
+    slots = lax.axis_size(across)
+    everything = vec
+    y = lambda arr_now: [(dev, dev ^ arr_now) for dev in range(slots)]
+    for i0 in range(slots.bit_length() - 1):
+        inter = y(1 << i0)
+        far_arr = lax.ppermute(everything, across, perm=inter)
+        everything = everything + far_arr
+    return everything
+
+
+move_lines = functools.partial(build_stocks_over_axis, across="rep")
 
 
 def adagrad(table_rows, accum_rows, gradient):
@@ -26,7 +41,7 @@
     dense = jax.ops.segment_sum(hot_grads.astype(jnp.float32), hot_ids, num_segments=hot_count)
     share = hot_count // lax.axis_size("shard")
     part_sum = lax.psum_scatter(dense, "shard", scatter_dimension=0, tiled=True)
-    part_sum = lax.psum(part_sum, "rep")
+    part_sum = move_lines(part_sum)
     start = lax.axis_index("shard") * share
     rows_share = lax.dynamic_slice_in_dim(hot_rows, start, share, 0)
     accum_share = lax.dynamic_slice_in_dim(hot_accum, start, share, 0)

time: 200 us -> 180 us (0.900)
  waiting for transfers between devices: 116 us -> 89.3 us
  starting transfers between devices: 7.29 us -> 13.4 us
    psum x1 -> x0, waiting for transfers between devices: 46.8 us -> none  [local(): part_sum = lax.psum(part_sum, 'rep')]
    ppermute x0 -> x2, waiting for transfers between devices: none -> 20 us  [build_stocks_over_axis(): far_arr = lax.ppermute(everything, across, perm=inter)]
    all_to_all x1, starting transfers between devices: 4.6 us -> 7.72 us  [local(): lax.all_to_all(cold_counts, ('rep', 'shard'), split_axis=1, concat_axis=0...]
    ppermute x0 -> x2, starting transfers between devices: none -> 2.99 us  [build_stocks_over_axis(): far_arr = lax.ppermute(everything, across, perm=inter)]
  transfers between devices with their start and end apart: 5 -> 6, of which waited for: 4 -> 5; matrix products, arithmetic and copies ran while one was open for 8% -> 9% of each run, Pallas kernels for 0% -> 0%
where the time goes in v1:
time: 180 us; the launch traced here: 179 us
  waiting for transfers between devices  89.3 us (50%)
  other arithmetic  32.5 us (18%)
  blocking collectives  23.2 us (13%)
  between operations  14.1 us (8%)
  starting transfers between devices  13.4 us (7%)
  local copies, waits for them, and re-layouts  6.56 us (4%)
    reduce_scatter x1, waiting for transfers between devices, local(): part_sum = lax.psum_scatter(dense, 'shard', scatter_dimension=0, tiled=True)  52.8 us
    ppermute x2, waiting for transfers between devices, build_stocks_over_axis(): far_arr = lax.ppermute(everything, across, perm=inter)  20 us
    scatter-add x1, other arithmetic, local(): jax.ops.segment_sum(hot_grads.astype(jnp.float32), hot_ids, num_segments=...  14.1 us
    all_gather x1, blocking collectives, local(): lax.all_gather(accum_new, 'shard', axis=0, tiled=True)  14.1 us
    all_to_all x1, waiting for transfers between devices, local(): lax.all_to_all(cold_grads, ('rep', 'shard'), split_axis=1, concat_axis=0,...  9.51 us
    all_to_all x1, blocking collectives, local(): lax.all_to_all(cold_slots, ('rep', 'shard'), split_axis=1, concat_axis=0,...  9.13 us
    all_to_all x1, starting transfers between devices, local(): lax.all_to_all(cold_counts, ('rep', 'shard'), split_axis=1, concat_axis=0...  7.72 us
    all_to_all x1, waiting for transfers between devices, local(): lax.all_to_all(cold_counts, ('rep', 'shard'), split_axis=1, concat_axis=0...  7.02 us
  transfers between devices with their start and end apart: 6, of which 5 were waited for; matrix products, arithmetic and copies ran while one was open for 9% of the time, Pallas kernels for 0%

profile of v1, /device:TPU:0, one launch (start us, length us, event | category | flops | bytes accessed | tf_op | source)
XLA Modules:
  0.0 179.1 jit_solution(8736421293171864418)
XLA Ops:
  7.2 0.0 reduce-scatter.2.cloned.1.call-start
  7.2 14.1 %scatter_custom_fusion = f32[8192,128]{1,0:T(8,128)} fusion(s32[2048]{0:T(1024)} %param.9, f32[]{:T(128)} %constant.3.clone.1, bf16[2048,128]{1,0:T(8,128)(2,1)} %param.10), kind=kCustom, calls=%fused_computation.6 | custom fusion | flops 524288 | bytes 4719104 | tf_op jit(solution)/shard_map/scatter-add | solution.py:41
  21.3 0.0 all-gather.2.cloned.1.call-start
  21.4 52.8 %reduce-scatter.2.cloned.1.call-done = f32[1024,128]{1,0:T(8,128)} async-done(((f32[8192,128]{1,0:T(8,128)}), f32[1024,128]{1,0:T(8,128)}) %reduce-scatter.2.cloned.1.call-update) | async-done | bytes 524304 | tf_op jit(solution)/shard_map/reduce_scatter | solution.py:43
  74.1 1.5 collective-permute-start
  75.6 10.6 %collective-permute-done = f32[1024,128]{1,0:T(8,128)S(1)} collective-permute-done((f32[1024,128]{1,0:T(8,128)}, f32[1024,128]{1,0:T(8,128)S(1)}, u32[]{:S(2)}, u32[]{:S(2)}) %collective-permute-start) | collective-permute-done | bytes 524320 | tf_op jit(solution)/shard_map/ppermute | solution.py:16
  86.1 1.1 add.23
  87.3 1.5 collective-permute-start.1
  88.8 9.5 %collective-permute-done.1 = f32[1024,128]{1,0:T(8,128)S(1)} collective-permute-done((f32[1024,128]{1,0:T(8,128)S(1)}, f32[1024,128]{1,0:T(8,128)S(1)}, u32[]{:S(2)}, u32[]{:S(2)}) %collective-permute-start.1) | collective-permute-done | bytes 524320 | tf_op jit(solution)/shard_map/ppermute | solution.py:16
  98.3 0.2 multiply_reduce_fusion.1
  98.5 0.7 fusion.8
  99.2 2.0 %divide_subtract_fusion.1 = f32[1024,128]{1,0:T(8,128)} fusion(f32[8192,128]{1,0:T(8,128)} %param.11, s32[]{:T(128)S(6)} %select_n.11, f32[1024]{0:T(1024)S(1)} %get-tuple-element.6, f32[1024,128]{1,0:T(8,128)S(1)} %add.23, f32[1024,128]{1,0:T(8,128)S(1)} %collective-permute-done.1), kind=kLoop, calls=%fused_computation.9 | loop fusion | flops 524288 | bytes 2101252 | tf_op jit(solution)/shard_map/sub | solution.py:26
  101.3 0.7 copy.18
  102.0 7.7 %all-to-all-start.1 = ((s32[1,32,1]{2,0,1:T(1,128)}), s32[1,32,1]{2,0,1:T(1,128)S(1)}, u32[]{:S(2)}, u32[]{:S(2)}) async-start(s32[1,32,1]{2,0,1:T(1,128)} %copy.18), calls=%async_computation.2 | async-start | bytes 32768 | tf_op jit(solution)/shard_map/all_to_all | solution.py:56
  109.7 0.1 copy.17
  109.8 7.0 %all-to-all-done.1 = s32[1,32,1]{2,0,1:T(1,128)S(1)} async-done(((s32[1,32,1]{2,0,1:T(1,128)}), s32[1,32,1]{2,0,1:T(1,128)S(1)}, u32[]{:S(2)}, u32[]{:S(2)}) %all-to-all-start.1) | async-done | bytes 160 | tf_op jit(solution)/shard_map/all_to_all | solution.py:56
  116.8 9.1 %all_to_all.31 = s32[1,32,16]{2,0,1:T(1,128)S(1)} all-to-all(s32[1,32,16]{2,0,1:T(1,128)S(1)} %copy.17), channel_id=1, replica_groups=mesh['rep'=4,'shard'=8] {'rep','shard'}, dimensions={1} | all-to-all | bytes 4096 | tf_op jit(solution)/shard_map/all_to_all | solution.py:55
  125.9 2.6 %all-to-all-start.2 = ((bf16[1,32,16,128]{3,2,0,1:T(8,128)(2,1)}), bf16[1,32,16,128]{3,2,0,1:T(8,128)(2,1)S(1)}, u32[]{:S(2)}, u32[]{:S(2)}) async-start(bf16[1,32,16,128]{3,2,0,1:T(8,128)(2,1)} %bitcast.1), calls=%async_computation.3 | async-start | bytes 262144 | tf_op jit(solution)/shard_map/all_to_all | solution.py:54
  128.5 0.7 reduce.1
  129.2 0.1 iota_compare_fusion
  129.2 0.1 lt.33
  129.3 0.5 broadcast.40
  129.9 0.7 reduce.4
  130.6 0.1 reshape.77
  130.6 9.5 %all-to-all-done.2 = bf16[1,32,16,128]{3,2,0,1:T(8,128)(2,1)S(1)} async-done(((bf16[1,32,16,128]{3,2,0,1:T(8,128)(2,1)}), bf16[1,32,16,128]{3,2,0,1:T(8,128)(2,1)S(1)}, u32[]{:S(2)}, u32[]{:S(2)}) %all-to-all-start.2) | async-done | bytes 131104 | tf_op jit(solution)/shard_map/all_to_all | solution.py:54
  140.1 4.6 %scatter_custom_fusion.1 = f32[8192,128]{1,0:T(8,128)} fusion(s32[512]{0:T(512)S(1)} %reshape.77, f32[]{:T(128)} %constant.3.clone.1, bf16[512,128]{1,0:T(8,128)(2,1)S(1)} %bitcast.7, pred[512]{0:T(512)(128)(4,1)S(1)} %lt.33), kind=kCustom, calls=%fused_computation.4 | custom fusion | flops 196608 | bytes 4326912 | tf_op jit(solution)/shard_map/scatter-add | solution.py:64
  144.8 3.5 %multiply_reduce_fusion = f32[8192]{0:T(1024)S(1)} fusion(f32[8192,128]{1,0:T(8,128)} %scatter_custom_fusion.1), kind=kLoop, calls=%fused_computation.3 | loop fusion | flops 2088960 | bytes 4227072 | tf_op jit(solution)/shard_map/reduce_sum | solution.py:25
  148.3 0.6 fusion.7
  148.9 4.2 %divide_subtract_fusion = f32[8192,128]{1,0:T(8,128)} fusion(f32[8192,128]{1,0:T(8,128)} %param.16, f32[8192,128]{1,0:T(8,128)S(1)} %copy-done, f32[8192]{0:T(1024)S(1)} %get-tuple-element.4), kind=kLoop, calls=%fused_computation.2 | loop fusion | flops 3145728 | bytes 12615680 | tf_op jit(solution)/shard_map/sub | solution.py:26
  153.1 14.1 %all_gather.7 = f32[8192]{0:T(1024)S(1)} all-gather(f32[1024]{0:T(1024)S(1)} %get-tuple-element.7), channel_id=1, replica_groups=mesh['rep'=4,'shard'=8] {'shard'}, dimensions={0}, use_global_device_ids=true | all-gather | bytes 36864 | tf_op jit(solution)/shard_map/all_gather | solution.py:51
  167.2 4.5 %copy.22 = f32[8192,128]{1,0:T(8,128)} copy(f32[8192,128]{1,0:T(8,128)} %all-gather.2.cloned.1.call-done) | data formatting | bytes 8388608
  171.6 0.6 copy.23
  (11 shorter events, 0.0 us)
Async XLA Ops:
  7.2 67.0 %reduce-scatter.2.cloned.1.call-start = ((), (), s32[]{:S(2)}) async-start(), calls=%async_computation.4 | async-start | bytes 4718592 | tf_op jit(solution)/shard_map/reduce_scatter | solution.py:43
  21.3 80.0 %copy-start.3 = (s32[1,32]{1,0:T(1,128)S(1)}, s32[1,32]{1,0:T(1,128)}, u32[]{:S(2)}) copy-start(s32[1,32]{1,0:T(1,128)} %param.13) | copy-start | bytes 388
  21.3 88.4 %copy-start.2 = (s32[1,32,16]{1,2,0:T(8,128)S(1)}, s32[1,32,16]{1,2,0:T(8,128)}, u32[]{:S(2)}) copy-start(s32[1,32,16]{1,2,0:T(8,128)} %param.14) | copy-start | bytes 6148
  21.3 145.8 %all-gather.2.cloned.1.call-start = ((), (), s32[]{:S(2)}) async-start(), calls=%async_computation.5 | async-start | bytes 4718592 | tf_op jit(solution)/shard_map/all_gather | solution.py:50
  74.1 12.0 %collective-permute-start = (f32[1024,128]{1,0:T(8,128)}, f32[1024,128]{1,0:T(8,128)S(1)}, u32[]{:S(2)}, u32[]{:S(2)}) collective-permute-start(f32[1024,128]{1,0:T(8,128)} %reduce-scatter.2.cloned.1.call-done), channel_id=1, source_target_pairs={{0,8},{8,0},{16,24},{24,16},{1,9},{9,1},{17,25},{25,17},{2,10},{10... | collective-permute-start | bytes 1572872 | tf_op jit(solution)/shard_map/ppermute | solution.py:16
  87.3 11.0 %collective-permute-start.1 = (f32[1024,128]{1,0:T(8,128)S(1)}, f32[1024,128]{1,0:T(8,128)S(1)}, u32[]{:S(2)}, u32[]{:S(2)}) collective-permute-start(f32[1024,128]{1,0:T(8,128)S(1)} %add.23), channel_id=1, source_target_pairs={{0,16},{8,24},{16,0},{24,8},{1,17},{9,25},{17,1},{25,9},{2,18},{10... | collective-permute-start | bytes 1572872 | tf_op jit(solution)/shard_map/ppermute | solution.py:16
  102.0 14.8 %all-to-all-start.1 = ((s32[1,32,1]{2,0,1:T(1,128)}), s32[1,32,1]{2,0,1:T(1,128)S(1)}, u32[]{:S(2)}, u32[]{:S(2)}) async-start(s32[1,32,1]{2,0,1:T(1,128)} %copy.18), calls=%async_computation.2 | async-start | bytes 32768 | tf_op jit(solution)/shard_map/all_to_all | solution.py:56
  125.9 14.2 %all-to-all-start.2 = ((bf16[1,32,16,128]{3,2,0,1:T(8,128)(2,1)}), bf16[1,32,16,128]{3,2,0,1:T(8,128)(2,1)S(1)}, u32[]{:S(2)}, u32[]{:S(2)}) async-start(bf16[1,32,16,128]{3,2,0,1:T(8,128)(2,1)} %bitcast.1), calls=%async_computation.3 | async-start | bytes 262144 | tf_op jit(solution)/shard_map/all_to_all | solution.py:54
  140.1 8.1 %copy-start.1 = (f32[8192]{0:T(1024)S(1)}, f32[8192]{0:T(1024)}, u32[]{:S(2)}) copy-start(f32[8192]{0:T(1024)} %param.17) | copy-start | bytes 98308
  144.7 4.1 %copy-start = (f32[8192,128]{1,0:T(8,128)S(1)}, f32[8192,128]{1,0:T(8,128)}, u32[]{:S(2)}) copy-start(f32[8192,128]{1,0:T(8,128)} %scatter_custom_fusion.1) | copy-start | bytes 12582916
Sparse Core Ops, SparseCore 0:
  21.4 52.6 reduce-scatter.1
  101.4 53.1 all-gather.1
